TPU v7x, 32 devices: a whole 2x2x4 slice. The times are simulated.
32 devices in a mesh: shard: 8 (over z, y), tensor: 2 (over core), context: 2 (over x).
Axes of the slice: x: 2, y: 2, z: 4, core: 2. Of those that a mesh axis runs over, the one named last changes fastest.
Arguments:
- hidden_in: bfloat16 [16, 1024, 1280], P(('shard', 'tensor'), 'context'), may hold values from -6 to 6
- patch_rows: int32 [16, 1024], P('shard', 'context'), may hold values from 0 to 63
- patch_cols: int32 [16, 1024], P('shard', 'context'), may hold values from 0 to 63
- attn_norm_gain: float32 [1280], replicated, may hold values from 0.5 to 1.5
- attn_norm_bias: float32 [1280], replicated, may hold values from -1.2 to 1.2
- query_key_value_weight: bfloat16 [1280, 3, 1280], P(('shard', 'context'), None, 'tensor'), may hold values from -0.15625 to 0.15625
- query_key_value_bias: float32 [3, 1280], replicated, may hold values from -1.2 to 1.2
- out_weight: bfloat16 [1280, 1280], P('tensor', ('shard', 'context')), may hold values from -2.5 to 2.5
- out_bias: float32 [1280], replicated, may hold values from -1.2 to 1.2
- mlp_norm_gain: float32 [1280], replicated, may hold values from 0.5 to 1.5
- mlp_norm_bias: float32 [1280], replicated, may hold values from -1.2 to 1.2
- fc1_weight: bfloat16 [1280, 5120], P(('shard', 'context'), 'tensor'), may hold values from -0.15625 to 0.15625
- fc1_bias: float32 [5120], replicated, may hold values from -1.2 to 1.2
- fc2_weight: bfloat16 [5120, 1280], P('tensor', ('shard', 'context')), may hold values from -0.078125 to 0.078125
- fc2_bias: float32 [1280], replicated, may hold values from -1.2 to 1.2
- cotangent: bfloat16 [16, 1024, 1280], P(('shard', 'tensor'), 'context'), may hold values from -6 to 6
Outputs:
- block_out: bfloat16 [16, 1024, 1280], P(('shard', 'tensor'), 'context')
- grad_input: float32 [16, 1024, 1280], P(('shard', 'tensor'), 'context')
- grad_attn_norm_gain: float32 [1280], replicated
- grad_attn_norm_bias: float32 [1280], replicated
- grad_qkv_weight: float32 [1280, 3, 1280], P(('shard', 'context'), None, 'tensor')
- grad_qkv_bias: float32 [3, 1280], replicated
- grad_out_weight: float32 [1280, 1280], P('tensor', ('shard', 'context'))
- grad_out_bias: float32 [1280], replicated
- grad_mlp_norm_gain: float32 [1280], replicated
- grad_mlp_norm_bias: float32 [1280], replicated
- grad_fc1_weight: float32 [1280, 5120], P(('shard', 'context'), 'tensor')
- grad_fc1_bias: float32 [5120], replicated
- grad_fc2_weight: float32 [5120, 1280], P('tensor', ('shard', 'context'))
- grad_fc2_bias: float32 [1280], replicated
All inputs are finite; a program needn't handle non-finite values.
Results may differ from a plain program's by a relative error of at most 0.015.
Values may be sent and summed in bfloat16 or wider, within the bound.
A program may use at most 192 MiB of HBM per device.

v0:
```python
import jax
import jax.numpy as jnp
from jax import lax
from jax.sharding import PartitionSpec as P

HEAD_DIM = 80


def normalize(field, gain, shift):
    mean_value = jnp.mean(field, axis=-1, keepdims=True)
    centered = field - mean_value
    variance = jnp.mean(centered * centered, axis=-1, keepdims=True)
    inv_scale = lax.rsqrt(variance + 1e-06)
    unit_field = centered * inv_scale
    return (unit_field * gain + shift, unit_field, inv_scale)


def norm_backward(grad_normed, unit_field, inv_scale, gain):
    grad_unit = grad_normed * gain
    mean_grad = jnp.mean(grad_unit, axis=-1, keepdims=True)
    mean_along = jnp.mean(grad_unit * unit_field, axis=-1, keepdims=True)
    grad_field = inv_scale * (grad_unit - mean_grad - unit_field * mean_along)
    return (
        grad_field,
        jnp.sum(grad_normed * unit_field, axis=(0, 1)),
        jnp.sum(grad_normed, axis=(0, 1)),
    )


def rotary_tables(rows_index, cols_index):
    quarter = HEAD_DIM // 4
    frequency = 10000.0 ** (-jnp.arange(quarter, dtype=jnp.float32) / quarter)
    row_angles = rows_index.astype(jnp.float32)[..., None] * frequency
    col_angles = cols_index.astype(jnp.float32)[..., None] * frequency
    angles = jnp.concatenate([row_angles, col_angles, row_angles, col_angles], axis=-1)
    return (jnp.cos(angles)[:, :, None, :], jnp.sin(angles)[:, :, None, :])


def rotate(field, cosine, sine):
    middle_index = field.shape[-1] // 2
    turned = jnp.concatenate([-field[..., middle_index:], field[..., :middle_index]], axis=-1)
    return field * cosine + turned * sine


def rotate_back(grad_field, cosine, sine):
    middle_index = grad_field.shape[-1] // 2
    weighted = grad_field * sine
    turned = jnp.concatenate([weighted[..., middle_index:], -weighted[..., :middle_index]], axis=-1)
    return grad_field * cosine + turned


def attend_forward(inputs):
    queries, keys, values = inputs
    scores = jnp.einsum(
        "phd,khd->hpk", queries, keys, preferred_element_type=jnp.float32
    ) * HEAD_DIM ** (-0.5)
    row_top = jnp.max(scores, axis=-1, keepdims=True)
    expos = jnp.exp(scores - row_top)
    row_total = jnp.sum(expos, axis=-1, keepdims=True)
    weights = (expos / row_total).astype(jnp.bfloat16)
    mixed = jnp.einsum("hpk,khd->phd", weights, values, preferred_element_type=jnp.float32)
    return (mixed, (row_top + jnp.log(row_total))[..., 0])


def attend_backward(inputs):
    queries, keys, values, log_total, grad_mixed = inputs
    scale_factor = HEAD_DIM ** (-0.5)
    scores = (
        jnp.einsum("phd,khd->hpk", queries, keys, preferred_element_type=jnp.float32) * scale_factor
    )
    probs = jnp.exp(scores - log_total[..., None])
    grad_probs = jnp.einsum("phd,khd->hpk", grad_mixed, values, preferred_element_type=jnp.float32)
    inner_sum = jnp.sum(probs * grad_probs, axis=-1, keepdims=True)
    grad_scores = (probs * (grad_probs - inner_sum)).astype(jnp.bfloat16)
    grad_queries = (
        jnp.einsum("hpk,khd->phd", grad_scores, keys, preferred_element_type=jnp.float32)
        * scale_factor
    )
    grad_keys = (
        jnp.einsum("hpk,phd->khd", grad_scores, queries, preferred_element_type=jnp.float32)
        * scale_factor
    )
    grad_values = jnp.einsum(
        "hpk,phd->khd", probs.astype(jnp.bfloat16), grad_mixed, preferred_element_type=jnp.float32
    )
    return (grad_queries, grad_keys, grad_values)


def on_device(
    hidden_in,
    patch_rows,
    patch_cols,
    attn_norm_gain,
    attn_norm_bias,
    query_key_value_weight,
    query_key_value_bias,
    out_weight,
    out_bias,
    mlp_norm_gain,
    mlp_norm_bias,
    fc1_weight,
    fc1_bias,
    fc2_weight,
    fc2_bias,
    cotangent,
):
    local_width = query_key_value_weight.shape[2]
    local_units = fc1_weight.shape[1]
    head_count = local_width // HEAD_DIM
    tensor_rank = lax.axis_index("tensor")
    complete_query_key_value, full_out, full_fc1, full_fc2 = (
        lax.all_gather(query_key_value_weight, ("shard", "context"), axis=0, tiled=True),
        lax.all_gather(out_weight, ("shard", "context"), axis=1, tiled=True),
        lax.all_gather(fc1_weight, ("shard", "context"), axis=0, tiled=True),
        lax.all_gather(fc2_weight, ("shard", "context"), axis=1, tiled=True),
    )
    resid = hidden_in.astype(jnp.float32)
    normed_one, unit_one, scale_one = normalize(resid, attn_norm_gain, attn_norm_bias)
    collected_first_normed = lax.all_gather(
        normed_one.astype(jnp.bfloat16), "tensor", axis=0, tiled=True
    )
    group_images = collected_first_normed.shape[0]
    local_patches = collected_first_normed.shape[1]
    head_shape = (group_images, local_patches, head_count, HEAD_DIM)
    own_qkv_bias = lax.dynamic_slice_in_dim(
        query_key_value_bias, tensor_rank * local_width, local_width, 1
    )
    projection_output = (
        jnp.einsum(
            "bxv,vhl->bxhl",
            collected_first_normed,
            complete_query_key_value,
            preferred_element_type=jnp.float32,
        )
        + own_qkv_bias
    )
    cosine, sine = rotary_tables(patch_rows, patch_cols)
    queries = rotate(projection_output[:, :, 0].reshape(head_shape), cosine, sine).astype(
        jnp.bfloat16
    )
    keys_local = rotate(projection_output[:, :, 1].reshape(head_shape), cosine, sine).astype(
        jnp.bfloat16
    )
    values_local = projection_output[:, :, 2].astype(jnp.bfloat16)
    keys_flat = keys_local.reshape(group_images, local_patches, local_width)
    all_keys, all_values = (
        lax.all_gather(keys_flat, "context", axis=1, tiled=True),
        lax.all_gather(values_local, "context", axis=1, tiled=True),
    )
    image_patches = all_keys.shape[1]
    full_head_shape = (group_images, image_patches, head_count, HEAD_DIM)
    keys_heads = all_keys.reshape(full_head_shape)
    values_heads = all_values.reshape(full_head_shape)
    mixed_heads, log_total = lax.map(attend_forward, (queries, keys_heads, values_heads))
    attn_mixed = mixed_heads.reshape(group_images, local_patches, local_width).astype(jnp.bfloat16)
    shard_portion = attn_mixed
    attn_branch = lax.psum_scatter(
        jnp.einsum(
            "npe,ed->npd", shard_portion, full_out, preferred_element_type=jnp.float32
        ).astype(jnp.bfloat16),
        "tensor",
        scatter_dimension=0,
        tiled=True,
    ).astype(jnp.float32)
    middle = resid + attn_branch + out_bias
    normed_two, unit_two, scale_two = normalize(middle, mlp_norm_gain, mlp_norm_bias)
    gathered_two = lax.all_gather(normed_two.astype(jnp.bfloat16), "tensor", axis=0, tiled=True)
    own_fc1_bias = lax.dynamic_slice_in_dim(fc1_bias, tensor_rank * local_units, local_units, 0)
    pre_act = (
        jnp.einsum("npd,df->npf", gathered_two, full_fc1, preferred_element_type=jnp.float32)
        + own_fc1_bias
    )
    gate_sigmoid = jax.nn.sigmoid(1.702 * pre_act)
    activated = (pre_act * gate_sigmoid).astype(jnp.bfloat16)
    shard_portion = activated
    mlp_branch = lax.psum_scatter(
        jnp.einsum(
            "npf,fd->npd", shard_portion, full_fc2, preferred_element_type=jnp.float32
        ).astype(jnp.bfloat16),
        "tensor",
        scatter_dimension=0,
        tiled=True,
    ).astype(jnp.float32)
    block_out = (middle + mlp_branch + fc2_bias).astype(jnp.bfloat16)
    backward_query_key_value, back_out, back_fc1, back_fc2 = (
        lax.all_gather(query_key_value_weight, ("shard", "context"), axis=0, tiled=True),
        lax.all_gather(out_weight, ("shard", "context"), axis=1, tiled=True),
        lax.all_gather(fc1_weight, ("shard", "context"), axis=0, tiled=True),
        lax.all_gather(fc2_weight, ("shard", "context"), axis=1, tiled=True),
    )
    grad_top = cotangent.astype(jnp.float32)
    fc2_bias_part = jnp.sum(grad_top, axis=(0, 1))
    grad_gathered = lax.all_gather(cotangent, "tensor", axis=0, tiled=True)
    fc2_weight_part = jnp.einsum(
        "npf,npd->fd", activated, grad_gathered, preferred_element_type=jnp.float32
    )
    grad_act = jnp.einsum(
        "npd,fd->npf", grad_gathered, back_fc2, preferred_element_type=jnp.float32
    )
    slope = gate_sigmoid + 1.702 * pre_act * gate_sigmoid * (1.0 - gate_sigmoid)
    grad_pre = (grad_act * slope).astype(jnp.bfloat16)
    fc1_bias_own = jnp.sum(grad_pre, axis=(0, 1), dtype=jnp.float32)
    fc1_weight_part = jnp.einsum(
        "npd,npf->df", gathered_two, grad_pre, preferred_element_type=jnp.float32
    )
    shard_portion = grad_pre
    grad_normed_two = lax.psum_scatter(
        jnp.einsum(
            "npf,df->npd", shard_portion, back_fc1, preferred_element_type=jnp.float32
        ).astype(jnp.bfloat16),
        "tensor",
        scatter_dimension=0,
        tiled=True,
    ).astype(jnp.float32)
    grad_mid_norm, gain_two_part, shift_two_part = norm_backward(
        grad_normed_two, unit_two, scale_two, mlp_norm_gain
    )
    grad_middle = grad_top + grad_mid_norm
    out_bias_part = jnp.sum(grad_middle, axis=(0, 1))
    grad_mid_gathered = lax.all_gather(
        grad_middle.astype(jnp.bfloat16), "tensor", axis=0, tiled=True
    )
    out_weight_part = jnp.einsum(
        "npe,npd->ed", attn_mixed, grad_mid_gathered, preferred_element_type=jnp.float32
    )
    grad_mixed = jnp.einsum(
        "npd,ed->npe", grad_mid_gathered, back_out, preferred_element_type=jnp.float32
    ).astype(jnp.bfloat16)
    grad_queries, grad_keys_all, grad_values_all = lax.map(
        attend_backward,
        (queries, keys_heads, values_heads, log_total, grad_mixed.reshape(head_shape)),
    )
    grad_keys_own, grad_values_own = (
        lax.psum_scatter(
            grad_keys_all.reshape(group_images, image_patches, local_width).astype(jnp.bfloat16),
            "context",
            scatter_dimension=1,
            tiled=True,
        ).astype(jnp.float32),
        lax.psum_scatter(
            grad_values_all.reshape(group_images, image_patches, local_width).astype(jnp.bfloat16),
            "context",
            scatter_dimension=1,
            tiled=True,
        ).astype(jnp.float32),
    )
    grad_queries_pre = rotate_back(grad_queries, cosine, sine).reshape(
        group_images, local_patches, local_width
    )
    grad_keys_pre = rotate_back(grad_keys_own.reshape(head_shape), cosine, sine).reshape(
        group_images, local_patches, local_width
    )
    gradient_of_projection_output = jnp.stack(
        [grad_queries_pre, grad_keys_pre, grad_values_own], axis=2
    ).astype(jnp.bfloat16)
    qkv_bias_own = jnp.sum(gradient_of_projection_output, axis=(0, 1), dtype=jnp.float32)
    qkv_weight_part = jnp.einsum(
        "brj,brto->jto",
        collected_first_normed,
        gradient_of_projection_output,
        preferred_element_type=jnp.float32,
    )
    shard_portion = gradient_of_projection_output
    grad_normed_one = lax.psum_scatter(
        jnp.einsum(
            "ufzc,lzc->ufl",
            shard_portion,
            backward_query_key_value,
            preferred_element_type=jnp.float32,
        ).astype(jnp.bfloat16),
        "tensor",
        scatter_dimension=0,
        tiled=True,
    ).astype(jnp.float32)
    grad_in_norm, gain_one_part, shift_one_part = norm_backward(
        grad_normed_one, unit_one, scale_one, attn_norm_gain
    )
    grad_input = grad_middle + grad_in_norm
    grad_qkv_weight, grad_fc1_weight = (
        lax.psum_scatter(qkv_weight_part, ("shard", "context"), scatter_dimension=0, tiled=True),
        lax.psum_scatter(fc1_weight_part, ("shard", "context"), scatter_dimension=0, tiled=True),
    )
    grad_out_weight, grad_fc2_weight = (
        lax.psum_scatter(out_weight_part, ("shard", "context"), scatter_dimension=1, tiled=True),
        lax.psum_scatter(fc2_weight_part, ("shard", "context"), scatter_dimension=1, tiled=True),
    )
    qkv_bias_slot = lax.dynamic_update_slice_in_dim(
        jnp.zeros_like(query_key_value_bias), qkv_bias_own, tensor_rank * local_width, 1
    )
    fc1_bias_slot = lax.dynamic_update_slice_in_dim(
        jnp.zeros_like(fc1_bias), fc1_bias_own, tensor_rank * local_units, 0
    )
    (
        grad_attn_norm_gain,
        grad_attn_norm_bias,
        grad_qkv_bias,
        grad_out_bias,
        grad_mlp_norm_gain,
        grad_mlp_norm_bias,
        grad_fc1_bias,
        grad_fc2_bias,
    ) = lax.psum(
        (
            gain_one_part,
            shift_one_part,
            qkv_bias_slot,
            out_bias_part,
            gain_two_part,
            shift_two_part,
            fc1_bias_slot,
            fc2_bias_part,
        ),
        ("shard", "tensor", "context"),
    )
    return (
        block_out,
        grad_input,
        grad_attn_norm_gain,
        grad_attn_norm_bias,
        grad_qkv_weight,
        grad_qkv_bias,
        grad_out_weight,
        grad_out_bias,
        grad_mlp_norm_gain,
        grad_mlp_norm_bias,
        grad_fc1_weight,
        grad_fc1_bias,
        grad_fc2_weight,
        grad_fc2_bias,
    )


def solution(mesh):
    placed = (
        P(("shard", "tensor"), "context", None),
        P("shard", "context"),
        P("shard", "context"),
        P(),
        P(),
        P(("shard", "context"), None, "tensor"),
        P(),
        P("tensor", ("shard", "context")),
        P(),
        P(),
        P(),
        P(("shard", "context"), "tensor"),
        P(),
        P("tensor", ("shard", "context")),
        P(),
        P(("shard", "tensor"), "context", None),
    )
    return jax.shard_map(
        on_device,
        mesh=mesh,
        in_specs=placed,
        out_specs=(
            P(("shard", "tensor"), "context", None),
            P(("shard", "tensor"), "context", None),
            P(),
            P(),
            P(("shard", "context"), None, "tensor"),
            P(),
            P("tensor", ("shard", "context")),
            P(),
            P(),
            P(),
            P(("shard", "context"), "tensor"),
            P(),
            P("tensor", ("shard", "context")),
            P(),
        ),
        check_vma=False,
    )
```

profile of v0, /device:TPU:10, one launch (start us, length us, event | category | flops | bytes accessed | tf_op | source)
XLA Modules:
  0.0 1782.6 jit_solution(12670248808709686272)
XLA Ops:
  13.8 12.1 all-gather.12.cloned.1.call-done
  25.9 85.0 %all-gather.14.cloned.1.call-done = bf16[1280,3,640]{2,0,1:T(8,128)(2,1)} async-done(((bf16[80,3,640]{2,0,1:T(8,128)(2,1)}), bf16[1280,3,640]{2,0,1:T(8,128)(2,1)}) %all-gather.14.cloned.1.call-update) | async-done | bytes 4915216 | tf_op jit(solution)/shard_map/all_gather | solution.py:112
  165.3 36.0 %all-gather.16.cloned.1.call-done = bf16[2,1024,640]{2,1,0:T(8,128)(2,1)} async-done(((bf16[2,512,640]{2,1,0:T(8,128)(2,1)}), bf16[2,1024,640]{2,1,0:T(8,128)(2,1)}) %all-gather.16.cloned.1.call-update) | async-done | bytes 2621456 | tf_op jit(solution)/shard_map/all_gather | solution.py:147
  204.3 24.4 %while.28 = (s32[]{:T(128)}, bf16[2,512,8,80]{1,3,2,0:T(8,128)(2,1)}, f32[2,8,512]{2,1,0:T(8,128)S(1)}, bf16[2,1024,8,80]{1,3,2,0:T(8,128)(2,1)}, bf16[2,512,8,8...) while((s32[]{:T(128)}, bf16[2,512,8,80]{1,3,2,0:T(8,128)(2,1)}, ...), condition=%wide.region_5.6_spmd.clone, body=%wide.region_2.5_spmd.sunk.clone | while | flops 1379921920 | bytes 65538156 | solution.py:154
  228.8 33.3 %all-gather.18.cloned.1.call-done = bf16[640,1280]{0,1:T(8,128)(2,1)} async-done(((bf16[640,80]{0,1:T(8,128)(2,1)}), bf16[640,1280]{0,1:T(8,128)(2,1)}) %all-gather.18.cloned.1.call-update) | async-done | bytes 1638416 | tf_op jit(solution)/shard_map/all_gather | solution.py:113
  285.2 92.4 %all-gather.22.cloned.1.call-done = bf16[1280,2560]{1,0:T(8,128)(2,1)} async-done(((bf16[80,2560]{1,0:T(8,128)(2,1)}), bf16[1280,2560]{1,0:T(8,128)(2,1)}) %all-gather.22.cloned.1.call-update) | async-done | bytes 6553616 | tf_op jit(solution)/shard_map/all_gather | solution.py:114
  377.6 12.6 all-gather.20.cloned.1.call-done
  390.3 12.7 fusion.50
  404.4 99.0 %all-gather.24.cloned.1.call-done = bf16[2560,1280]{0,1:T(8,128)(2,1)} async-done(((bf16[2560,80]{0,1:T(8,128)(2,1)}), bf16[2560,1280]{0,1:T(8,128)(2,1)}) %all-gather.24.cloned.1.call-update) | async-done | bytes 6553616 | tf_op jit(solution)/shard_map/all_gather | solution.py:115
  503.4 14.2 convert_reduce_fusion
  519.9 11.1 fusion.58
  531.1 14.1 fusion.61
  563.2 12.6 all-gather.28.cloned.1.call-done
  583.7 82.4 %while.29 = (s32[]{:T(128)}, f32[2,512,8,80]{1,3,2,0:T(8,128)}, bf16[2,1024,8,80]{1,3,2,0:T(8,128)(2,1)}, bf16[2,1024,8,80]{1,3,2,0:T(8,128)(2,1)}, bf16[2,1024,...) while((s32[]{:T(128)}, f32[2,512,8,80]{1,3,2,0:T(8,128)}, ...), condition=%wide.region_15.16_spmd.clone, body=%wide.region_13.15_spmd.sunk.clone | while | flops 3406753792 | bytes 225039664 | solution.py:229
  675.1 33.3 %reduce-scatter.17.cloned.1.call-done = bf16[2,512,640]{2,1,0:T(8,128)(2,1)} async-done(((bf16[2,1024,640]{2,1,0:T(8,128)(2,1)}), bf16[2,512,640]{2,1,0:T(8,128)(2,1)}) %reduce-scatter.17.cloned.1.call-update) | async-done | bytes 1310736 | tf_op jit(solution)/shard_map/reduce_scatter | solution.py:234
  730.3 18.5 %reduce-scatter.19.cloned.1.call-done = bf16[2,512,640]{2,1,0:T(8,128)(2,1)} async-done(((bf16[2,1024,640]{2,1,0:T(8,128)(2,1)}), bf16[2,512,640]{2,1,0:T(8,128)(2,1)}) %reduce-scatter.19.cloned.1.call-update) | async-done | bytes 1310736 | tf_op jit(solution)/shard_map/reduce_scatter | solution.py:240
  773.9 13.8 convolution_bitcast_fusion
  787.7 12.8 convolution_bitcast_fusion.1
  800.6 10.3 convolution_bitcast_fusion.2
  816.5 35.3 %reduce-scatter.25.cloned.1.call-done = f32[640,80]{0,1:T(8,128)} async-done(((f32[640,1280]{0,1:T(8,128)}), f32[640,80]{0,1:T(8,128)}) %reduce-scatter.25.cloned.1.call-update) | async-done | bytes 204816 | tf_op jit(solution)/shard_map/reduce_scatter | solution.py:284
  851.8 140.3 %all-reduce.3.cloned.1.call-done = (f32[1280]{0:T(1024)}, f32[1280]{0:T(1024)}, f32[3,1280]{1,0:T(4,128)}, f32[1280]{0:T(1024)}, f32[1280]{0:T(1024)}, /*index=5*/f32[1280]{0:T(1024)}, f32[5120]{0:T(1024)}, f32[1280]{0:T(1024)}) async-done(((f32[1280]{0:T(1024)}, f32[1280]{0:T(1024)}, f32[3,1280]{1,0:T(4,128)}, f32[1280]{0:T(1024)}, f32[1280]{0:T(1024)}, /*index=5*/f32[1280]{0:T(1024)}, f32[5120]{0:T(1024)}, ...) | async-done | bytes 66576 | tf_op jit(solution)/shard_map/psum | solution.py:302
  992.1 279.6 %reduce-scatter.29.cloned.1.call-done = f32[2560,80]{0,1:T(8,128)} async-done(((f32[2560,1280]{0,1:T(8,128)}), f32[2560,80]{0,1:T(8,128)}) %reduce-scatter.29.cloned.1.call-update) | async-done | bytes 819216 | tf_op jit(solution)/shard_map/reduce_scatter | solution.py:285
  1271.7 280.3 %reduce-scatter.27.cloned.1.call-done = f32[80,2560]{1,0:T(8,128)} async-done(((f32[1280,2560]{1,0:T(8,128)}), f32[80,2560]{1,0:T(8,128)}) %reduce-scatter.27.cloned.1.call-update) | async-done | bytes 819216 | tf_op jit(solution)/shard_map/reduce_scatter | solution.py:281
  1552.0 213.1 %reduce-scatter.23.cloned.1.call-done = f32[80,3,640]{2,0,1:T(8,128)} async-done(((f32[1280,3,640]{2,0,1:T(8,128)}), f32[80,3,640]{2,0,1:T(8,128)}) %reduce-scatter.23.cloned.1.call-update) | async-done | bytes 614416 | tf_op jit(solution)/shard_map/reduce_scatter | solution.py:280
  (253 shorter events, 294.8 us)
Async XLA Ops:
  7.2 18.7 %all-gather.12.cloned.1.call-start = ((), (), s32[]{:S(2)}) async-start(), calls=%async_computation.10 | async-start | bytes 3932160 | tf_op jit(solution)/shard_map/all_gather | solution.py:119
  13.0 97.9 %all-gather.14.cloned.1.call-start = ((), (), s32[]{:S(2)}) async-start(), calls=%async_computation.11 | async-start | bytes 5222400 | tf_op jit(solution)/shard_map/all_gather | solution.py:112
  13.7 147.2 %all-gather.30.cloned.1.call-start = ((), (), s32[]{:S(2)}) async-start(), calls=%async_computation.29 | async-start | bytes 3932160 | tf_op jit(solution)/shard_map/all_gather | solution.py:148
  124.0 77.4 %all-gather.16.cloned.1.call-start = ((), (), s32[]{:S(2)}) async-start(), calls=%async_computation.12 | async-start | bytes 3932160 | tf_op jit(solution)/shard_map/all_gather | solution.py:147
  150.5 111.6 %all-gather.18.cloned.1.call-start = ((), (), s32[]{:S(2)}) async-start(), calls=%async_computation.13 | async-start | bytes 1740800 | tf_op jit(solution)/shard_map/all_gather | solution.py:113
  151.1 127.4 %reduce-scatter.11.cloned.1.call-start = ((), (), s32[]{:S(2)}) async-start(), calls=%async_computation.14 | async-start | bytes 3932160 | tf_op jit(solution)/shard_map/reduce_scatter | solution.py:157
  267.8 109.8 %all-gather.22.cloned.1.call-start = ((), (), s32[]{:S(2)}) async-start(), calls=%async_computation.16 | async-start | bytes 6963200 | tf_op jit(solution)/shard_map/all_gather | solution.py:114
  268.6 121.7 %all-gather.20.cloned.1.call-start = ((), (), s32[]{:S(2)}) async-start(), calls=%async_computation.15 | async-start | bytes 3932160 | tf_op jit(solution)/shard_map/all_gather | solution.py:167
  283.6 120.8 %all-gather.26.cloned.1.call-start = ((), (), s32[]{:S(2)}) async-start(), calls=%async_computation.19 | async-start | bytes 3932160 | tf_op jit(solution)/shard_map/all_gather | solution.py:193
  284.3 219.1 %all-gather.24.cloned.1.call-start = ((), (), s32[]{:S(2)}) async-start(), calls=%async_computation.17 | async-start | bytes 6963200 | tf_op jit(solution)/shard_map/all_gather | solution.py:115
  284.9 260.8 %reduce-scatter.15.cloned.1.call-start = ((), (), s32[]{:S(2)}) async-start(), calls=%async_computation.20 | async-start | bytes 3932160 | tf_op jit(solution)/shard_map/reduce_scatter | solution.py:207
  285.2 245.9 %copy-start.37 = (f32[2560]{0:T(1024)}, f32[2560]{0:T(1024)S(1)}, u32[]{:S(2)}) copy-start(f32[2560]{0:T(1024)S(1)} %dynamic_slice.34) | copy-start | bytes 30724
  531.0 24.0 %reduce-scatter.13.cloned.1.call-start = ((), (), s32[]{:S(2)}) async-start(), calls=%async_computation.18 | async-start | bytes 3932160 | tf_op jit(solution)/shard_map/reduce_scatter | solution.py:176
  545.2 30.6 %all-gather.28.cloned.1.call-start = ((), (), s32[]{:S(2)}) async-start(), calls=%async_computation.21 | async-start | bytes 3932160 | tf_op jit(solution)/shard_map/all_gather | solution.py:220
  563.1 145.3 %reduce-scatter.17.cloned.1.call-start = ((), (), s32[]{:S(2)}) async-start(), calls=%async_computation.22 | async-start | bytes 3932160 | tf_op jit(solution)/shard_map/reduce_scatter | solution.py:234
  670.6 78.2 %reduce-scatter.19.cloned.1.call-start = ((), (), s32[]{:S(2)}) async-start(), calls=%async_computation.23 | async-start | bytes 3932160 | tf_op jit(solution)/shard_map/reduce_scatter | solution.py:240
  675.0 36.4 %copy-start.18 = (f32[2,512,8,80]{1,3,2,0:T(8,128)S(1)}, f32[2,512,8,80]{1,3,2,0:T(8,128)}, u32[]{:S(2)}) copy-start(f32[2,512,8,80]{1,3,2,0:T(8,128)} %get-tuple-element.98) | copy-start | bytes 7864324
  675.0 95.6 %reduce-scatter.21.cloned.1.call-start = ((), (), s32[]{:S(2)}) async-start(), calls=%async_computation.24 | async-start | bytes 3932160 | tf_op jit(solution)/shard_map/reduce_scatter | solution.py:264
  758.7 93.1 %reduce-scatter.25.cloned.1.call-start = ((), (), s32[]{:S(2)}) async-start(), calls=%async_computation.26 | async-start | bytes 3481600 | tf_op jit(solution)/shard_map/reduce_scatter | solution.py:284
  765.8 226.3 %all-reduce.3.cloned.1.call-start = ((), (), s32[]{:S(2)}) async-start(), calls=%async_computation.30 | async-start | bytes 180224 | tf_op jit(solution)/shard_map/psum | solution.py:302
  773.8 497.9 %reduce-scatter.29.cloned.1.call-start = ((), (), s32[]{:S(2)}) async-start(), calls=%async_computation.28 | async-start | bytes 13926400 | tf_op jit(solution)/shard_map/reduce_scatter | solution.py:285
  787.7 764.3 %reduce-scatter.27.cloned.1.call-start = ((), (), s32[]{:S(2)}) async-start(), calls=%async_computation.27 | async-start | bytes 13926400 | tf_op jit(solution)/shard_map/reduce_scatter | solution.py:281
  800.6 964.5 %reduce-scatter.23.cloned.1.call-start = ((), (), s32[]{:S(2)}) async-start(), calls=%async_computation.25 | async-start | bytes 10444800 | tf_op jit(solution)/shard_map/reduce_scatter | solution.py:280
  811.0 964.5 %copy-start.1 = (f32[3,1280]{1,0:T(4,128)S(1)}, f32[3,1280]{1,0:T(4,128)}, u32[]{:S(2)}) copy-start(f32[3,1280]{1,0:T(4,128)} %param.26) | copy-start | bytes 46084
  (52 other events, 265.2 us)
Sparse Core Ops, SparseCore 0:
  13.1 12.7 all-gather.11
  28.6 82.2 all-gather.13
  124.1 36.7 all-gather.29
  162.3 38.9 all-gather.15
  203.9 58.1 all-gather.17
  267.9 10.5 reduce-scatter.10
  281.2 96.4 all-gather.21
  379.8 10.4 all-gather.19
  391.8 12.5 all-gather.25
  406.9 96.4 all-gather.23
  531.1 9.7 reduce-scatter.14
  545.3 9.7 reduce-scatter.12
  563.2 12.5 all-gather.27
  670.7 37.6 reduce-scatter.16
  711.0 37.6 reduce-scatter.18
  758.8 11.7 reduce-scatter.20
  773.3 78.4 reduce-scatter.24
  859.2 132.8 all-reduce.2
  995.0 276.6 reduce-scatter.28
  1274.4 277.5 reduce-scatter.26
  1554.9 210.1 reduce-scatter.22
where the time goes:
time: 1790 us; the launch traced here: 1780 us
  waiting for transfers between devices  1410 us (79%)
  matrix products  195 us (11%)
  local copies, waits for them, and re-layouts  79.3 us (4%)
  other arithmetic  78.1 us (4%)
    reduce_scatter x1, waiting for transfers between devices, on_device(): lax.psum_scatter(fc1_weight_part, ('shard', 'context'), scatter_dimension...  280 us
    reduce_scatter x1, waiting for transfers between devices, on_device(): lax.psum_scatter(fc2_weight_part, ('shard', 'context'), scatter_dimension...  280 us
    reduce_scatter x1, waiting for transfers between devices, on_device(): lax.psum_scatter(qkv_weight_part, ('shard', 'context'), scatter_dimension...  213 us
    psum x1, waiting for transfers between devices, on_device(): lax.psum((gain_one_part, shift_one_part, qkv_bias_slot, out_bias_part, ga...  140 us
    all_gather x1, waiting for transfers between devices, on_device(): lax.all_gather(fc2_weight, ('shard', 'context'), axis=1, tiled=True)  99 us
    all_gather x1, waiting for transfers between devices, on_device(): lax.all_gather(fc1_weight, ('shard', 'context'), axis=0, tiled=True)  92.4 us
    all_gather x1, waiting for transfers between devices, on_device(): lax.all_gather(query_key_value_weight, ('shard', 'context'), axis=0, tile...  85 us
    all_gather x1, waiting for transfers between devices, on_device(): lax.all_gather(keys_flat, 'context', axis=1, tiled=True)  36 us
  transfers between devices with their start and end apart: 21, of which 20 were waited for; matrix products, arithmetic and copies ran while one was open for 10% of the time, Pallas kernels for 0%

commit v1 on v0

--- a/solution.py
+++ b/solution.py
@@ -4,6 +4,36 @@
 from jax.sharding import PartitionSpec as P
 
 HEAD_DIM = 80
+
+
+def lots_all_hold(buf):
+    mixed_arr = lax.axis_size(("shard", "context"))
+    last = lax.axis_index(("shard", "context"))
+    local_out, oldest, earlier = (mixed_arr, last, buf.shape[0])
+    everything = jnp.zeros(
+        [jj * local_out if hop_no == 0 else jj for hop_no, jj in enumerate(buf.shape)], buf.dtype
+    )
+    b_now = upper = buf
+    long_array = lax.dynamic_update_slice_in_dim(everything, buf, oldest * earlier, axis=0)
+    for at in range(1, local_out // 2 + 1):
+        b_now = lax.ppermute(
+            b_now,
+            axis_name=("shard", "context"),
+            perm=[(hop_no, (hop_no + 1) % local_out) for hop_no in range(local_out)],
+        )
+        long_array = lax.dynamic_update_slice_in_dim(
+            long_array, b_now, (oldest - at) % local_out * earlier, axis=0
+        )
+        if 2 * at < local_out:
+            upper = lax.ppermute(
+                upper,
+                axis_name=("shard", "context"),
+                perm=[(hop_no, (hop_no - 1) % local_out) for hop_no in range(local_out)],
+            )
+            long_array = lax.dynamic_update_slice_in_dim(
+                long_array, upper, (oldest + at) % local_out * earlier, axis=0
+            )
+    return long_array
 
 
 def normalize(field, gain, shift):
@@ -109,7 +139,7 @@
     head_count = local_width // HEAD_DIM
     tensor_rank = lax.axis_index("tensor")
     complete_query_key_value, full_out, full_fc1, full_fc2 = (
-        lax.all_gather(query_key_value_weight, ("shard", "context"), axis=0, tiled=True),
+        lots_all_hold(query_key_value_weight),
         lax.all_gather(out_weight, ("shard", "context"), axis=1, tiled=True),
         lax.all_gather(fc1_weight, ("shard", "context"), axis=0, tiled=True),
         lax.all_gather(fc2_weight, ("shard", "context"), axis=1, tiled=True),

time: 1790 us -> 1900 us (1.061)
  waiting for transfers between devices: 1410 us -> 1500 us
    ppermute x0 -> x15, waiting for transfers between devices: none -> 75.1 us  [the longest x8 74.7 us: lots_all_hold(): lax.ppermute(b_now, axis_name=('shard', 'context'), perm=[(hop_no, (hop_n...]
    all_gather x1, waiting for transfers between devices: 8.05 us -> 36.7 us  [on_device(): lax.all_gather(values_local, 'context', axis=1, tiled=True)]
    all_gather x1, waiting for transfers between devices: 85 us -> 62.7 us  [on_device(): lax.all_gather(query_key_value_weight, ('shard', 'context'), axis=0, tile...]
    reduce_scatter x1, waiting for transfers between devices: 18.5 us -> 38.1 us  [on_device(): lax.psum_scatter(grad_values_all.reshape(group_images, image_patches, loc...]
  transfers between devices with their start and end apart: 21 -> 36, of which waited for: 20 -> 28; matrix products, arithmetic and copies ran while one was open for 10% -> 9% of each run, Pallas kernels for 0% -> 0%
where the time goes in v1:
time: 1900 us; the launch traced here: 1890 us
  waiting for transfers between devices  1500 us (79%)
  matrix products  196 us (10%)
  local copies, waits for them, and re-layouts  88.8 us (5%)
  other arithmetic  78.4 us (4%)
    reduce_scatter x1, waiting for transfers between devices, on_device(): lax.psum_scatter(fc2_weight_part, ('shard', 'context'), scatter_dimension...  280 us
    reduce_scatter x1, waiting for transfers between devices, on_device(): lax.psum_scatter(fc1_weight_part, ('shard', 'context'), scatter_dimension...  280 us
    reduce_scatter x1, waiting for transfers between devices, on_device(): lax.psum_scatter(qkv_weight_part, ('shard', 'context'), scatter_dimension...  213 us
    psum x1, waiting for transfers between devices, on_device(): lax.psum((gain_one_part, shift_one_part, qkv_bias_slot, out_bias_part, ga...  140 us
    all_gather x1, waiting for transfers between devices, on_device(): lax.all_gather(fc2_weight, ('shard', 'context'), axis=1, tiled=True)  99.2 us
    all_gather x1, waiting for transfers between devices, on_device(): lax.all_gather(fc1_weight, ('shard', 'context'), axis=0, tiled=True)  92.7 us
    ppermute x8, waiting for transfers between devices, lots_all_hold(): lax.ppermute(b_now, axis_name=('shard', 'context'), perm=[(hop_no, (hop_n...  74.7 us
    all_gather x1, waiting for transfers between devices, on_device(): lax.all_gather(query_key_value_weight, ('shard', 'context'), axis=0, tile...  62.7 us
  transfers between devices with their start and end apart: 36, of which 28 were waited for; matrix products, arithmetic and copies ran while one was open for 9% of the time, Pallas kernels for 0%

profile of v1, /device:TPU:10, one launch (start us, length us, event | category | flops | bytes accessed | tf_op | source)
XLA Modules:
  0.0 1892.3 jit_solution(13902857124684935445)
XLA Ops:
  57.5 11.7 collective-permute-done.6
  105.2 11.3 collective-permute-done.12
  163.8 32.1 %all-gather.14.cloned.1.call-done = bf16[2,1024,640]{2,1,0:T(8,128)(2,1)} async-done(((bf16[2,512,640]{2,1,0:T(8,128)(2,1)}), bf16[2,1024,640]{2,1,0:T(8,128)(2,1)}) %all-gather.14.cloned.1.call-update) | async-done | bytes 2621456 | tf_op jit(solution)/shard_map/all_gather | solution.py:177
  200.4 36.7 %all-gather.30.cloned.1.call-done = bf16[2,1024,1,640]{3,1,2,0:T(8,128)(2,1)} async-done(((bf16[2,512,1,640]{3,1,2,0:T(8,128)(2,1)}), bf16[2,1024,1,640]{3,1,2,0:T(8,128)(2,1)}) %all-gather.30.cloned.1.call-update) | async-done | bytes 2621456 | tf_op jit(solution)/shard_map/all_gather | solution.py:178
  241.4 23.6 %while.28 = (s32[]{:T(128)}, bf16[2,512,8,80]{1,3,2,0:T(8,128)(2,1)S(1)}, f32[2,8,512]{2,1,0:T(8,128)S(1)}, bf16[2,1024,8,80]{1,3,2,0:T(8,128)(2,1)}, bf16[2,512...) while((s32[]{:T(128)}, bf16[2,512,8,80]{1,3,2,0:T(8,128)(2,1)S(1)}, ...), condition=%wide.region_5.6_spmd.clone, body=%wide.region_2.5_spmd.sunk.clone | while | flops 1379921920 | bytes 65538148 | solution.py:184
  265.0 32.8 %all-gather.16.cloned.1.call-done = bf16[640,1280]{0,1:T(8,128)(2,1)} async-done(((bf16[640,80]{0,1:T(8,128)(2,1)}), bf16[640,1280]{0,1:T(8,128)(2,1)}) %all-gather.16.cloned.1.call-update) | async-done | bytes 1638416 | tf_op jit(solution)/shard_map/all_gather | solution.py:143
  320.0 92.7 %all-gather.20.cloned.1.call-done = bf16[1280,2560]{1,0:T(8,128)(2,1)} async-done(((bf16[80,2560]{1,0:T(8,128)(2,1)}), bf16[1280,2560]{1,0:T(8,128)(2,1)}) %all-gather.20.cloned.1.call-update) | async-done | bytes 6553616 | tf_op jit(solution)/shard_map/all_gather | solution.py:144
  412.7 12.6 all-gather.18.cloned.1.call-done
  425.4 12.7 fusion.50
  439.5 99.2 %all-gather.22.cloned.1.call-done = bf16[2560,1280]{0,1:T(8,128)(2,1)} async-done(((bf16[2560,80]{0,1:T(8,128)(2,1)}), bf16[2560,1280]{0,1:T(8,128)(2,1)}) %all-gather.22.cloned.1.call-update) | async-done | bytes 6553616 | tf_op jit(solution)/shard_map/all_gather | solution.py:145
  538.6 14.2 convert_reduce_fusion
  566.3 14.1 fusion.61
  598.2 12.6 all-gather.26.cloned.1.call-done
  616.7 76.5 %while.29 = (s32[]{:T(128)}, f32[2,512,8,80]{1,3,2,0:T(8,128)}, bf16[2,1024,8,80]{1,3,2,0:T(8,128)(2,1)}, bf16[2,1024,8,80]{1,3,2,0:T(8,128)(2,1)}, bf16[2,1024,...) while((s32[]{:T(128)}, f32[2,512,8,80]{1,3,2,0:T(8,128)}, ...), condition=%wide.region_15.16_spmd.clone, body=%wide.region_13.15_spmd.sunk.clone | while | flops 3406753792 | bytes 204068080 | solution.py:259
  702.0 33.5 %reduce-scatter.17.cloned.1.call-done = bf16[2,512,640]{2,1,0:T(8,128)(2,1)} async-done(((bf16[2,1024,640]{2,1,0:T(8,128)(2,1)}), bf16[2,512,640]{2,1,0:T(8,128)(2,1)}) %reduce-scatter.17.cloned.1.call-update) | async-done | bytes 1310736 | tf_op jit(solution)/shard_map/reduce_scatter | solution.py:264
  757.6 62.7 %all-gather.28.cloned.1.call-done = bf16[1280,3,640]{2,0,1:T(8,128)(2,1)} async-done(((bf16[80,3,640]{2,0,1:T(8,128)(2,1)}), bf16[1280,3,640]{2,0,1:T(8,128)(2,1)}) %all-gather.28.cloned.1.call-update) | async-done | bytes 4915216 | tf_op jit(solution)/shard_map/all_gather | solution.py:216
  820.3 38.1 %reduce-scatter.19.cloned.1.call-done = bf16[2,512,640]{2,1,0:T(8,128)(2,1)} async-done(((bf16[2,1024,640]{2,1,0:T(8,128)(2,1)}), bf16[2,512,640]{2,1,0:T(8,128)(2,1)}) %reduce-scatter.19.cloned.1.call-update) | async-done | bytes 1310736 | tf_op jit(solution)/shard_map/reduce_scatter | solution.py:270
  883.6 13.1 convolution_bitcast_fusion.1
  897.5 13.6 convolution_bitcast_fusion
  926.9 35.5 %reduce-scatter.25.cloned.1.call-done = f32[640,80]{0,1:T(8,128)} async-done(((f32[640,1280]{0,1:T(8,128)}), f32[640,80]{0,1:T(8,128)}) %reduce-scatter.25.cloned.1.call-update) | async-done | bytes 204816 | tf_op jit(solution)/shard_map/reduce_scatter | solution.py:314
  962.4 139.5 %all-reduce.3.cloned.1.call-done = (f32[1280]{0:T(1024)}, f32[1280]{0:T(1024)}, f32[3,1280]{1,0:T(4,128)}, f32[1280]{0:T(1024)}, f32[1280]{0:T(1024)}, /*index=5*/f32[1280]{0:T(1024)}, f32[5120]{0:T(1024)}, f32[1280]{0:T(1024)}) async-done(((f32[1280]{0:T(1024)}, f32[1280]{0:T(1024)}, f32[3,1280]{1,0:T(4,128)}, f32[1280]{0:T(1024)}, f32[1280]{0:T(1024)}, /*index=5*/f32[1280]{0:T(1024)}, f32[5120]{0:T(1024)}, ...) | async-done | bytes 66576 | tf_op jit(solution)/shard_map/psum | solution.py:332
  1101.9 279.6 %reduce-scatter.27.cloned.1.call-done = f32[80,2560]{1,0:T(8,128)} async-done(((f32[1280,2560]{1,0:T(8,128)}), f32[80,2560]{1,0:T(8,128)}) %reduce-scatter.27.cloned.1.call-update) | async-done | bytes 819216 | tf_op jit(solution)/shard_map/reduce_scatter | solution.py:311
  1381.5 280.3 %reduce-scatter.29.cloned.1.call-done = f32[2560,80]{0,1:T(8,128)} async-done(((f32[2560,1280]{0,1:T(8,128)}), f32[2560,80]{0,1:T(8,128)}) %reduce-scatter.29.cloned.1.call-update) | async-done | bytes 819216 | tf_op jit(solution)/shard_map/reduce_scatter | solution.py:315
  1661.8 213.1 %reduce-scatter.23.cloned.1.call-done = f32[80,3,640]{2,0,1:T(8,128)} async-done(((f32[1280,3,640]{2,0,1:T(8,128)}), f32[80,3,640]{2,0,1:T(8,128)}) %reduce-scatter.23.cloned.1.call-update) | async-done | bytes 614416 | tf_op jit(solution)/shard_map/reduce_scatter | solution.py:310
  (300 shorter events, 385.1 us)
Async XLA Ops:
  7.2 117.2 %all-gather.12.cloned.1.call-start = ((), (), s32[]{:S(2)}) async-start(), calls=%async_computation.10 | async-start | bytes 3932160 | tf_op jit(solution)/shard_map/all_gather | solution.py:149
  8.8 16.5 collective-permute-start.1
  24.8 171.1 %all-gather.14.cloned.1.call-start = ((), (), s32[]{:S(2)}) async-start(), calls=%async_computation.11 | async-start | bytes 3932160 | tf_op jit(solution)/shard_map/all_gather | solution.py:177
  25.3 16.8 collective-permute-start.3
  53.7 18.8 collective-permute-start.7
  159.5 77.6 %all-gather.30.cloned.1.call-start = ((), (), s32[]{:S(2)}) async-start(), calls=%async_computation.29 | async-start | bytes 3932160 | tf_op jit(solution)/shard_map/all_gather | solution.py:178
  162.5 135.3 %all-gather.16.cloned.1.call-start = ((), (), s32[]{:S(2)}) async-start(), calls=%async_computation.12 | async-start | bytes 1740800 | tf_op jit(solution)/shard_map/all_gather | solution.py:143
  163.1 150.6 %reduce-scatter.11.cloned.1.call-start = ((), (), s32[]{:S(2)}) async-start(), calls=%async_computation.13 | async-start | bytes 3932160 | tf_op jit(solution)/shard_map/reduce_scatter | solution.py:187
  303.0 109.7 %all-gather.20.cloned.1.call-start = ((), (), s32[]{:S(2)}) async-start(), calls=%async_computation.15 | async-start | bytes 6963200 | tf_op jit(solution)/shard_map/all_gather | solution.py:144
  303.6 121.7 %all-gather.18.cloned.1.call-start = ((), (), s32[]{:S(2)}) async-start(), calls=%async_computation.14 | async-start | bytes 3932160 | tf_op jit(solution)/shard_map/all_gather | solution.py:197
  318.2 121.2 %all-gather.24.cloned.1.call-start = ((), (), s32[]{:S(2)}) async-start(), calls=%async_computation.18 | async-start | bytes 3932160 | tf_op jit(solution)/shard_map/all_gather | solution.py:223
  319.0 219.6 %all-gather.22.cloned.1.call-start = ((), (), s32[]{:S(2)}) async-start(), calls=%async_computation.16 | async-start | bytes 6963200 | tf_op jit(solution)/shard_map/all_gather | solution.py:145
  319.7 261.2 %reduce-scatter.15.cloned.1.call-start = ((), (), s32[]{:S(2)}) async-start(), calls=%async_computation.19 | async-start | bytes 3932160 | tf_op jit(solution)/shard_map/reduce_scatter | solution.py:237
  566.3 24.0 %reduce-scatter.13.cloned.1.call-start = ((), (), s32[]{:S(2)}) async-start(), calls=%async_computation.17 | async-start | bytes 3932160 | tf_op jit(solution)/shard_map/reduce_scatter | solution.py:206
  580.4 30.4 %all-gather.26.cloned.1.call-start = ((), (), s32[]{:S(2)}) async-start(), calls=%async_computation.20 | async-start | bytes 3932160 | tf_op jit(solution)/shard_map/all_gather | solution.py:250
  598.2 137.3 %reduce-scatter.17.cloned.1.call-start = ((), (), s32[]{:S(2)}) async-start(), calls=%async_computation.21 | async-start | bytes 3932160 | tf_op jit(solution)/shard_map/reduce_scatter | solution.py:264
  697.6 122.7 %all-gather.28.cloned.1.call-start = ((), (), s32[]{:S(2)}) async-start(), calls=%async_computation.23 | async-start | bytes 5222400 | tf_op jit(solution)/shard_map/all_gather | solution.py:216
  698.2 160.3 %reduce-scatter.19.cloned.1.call-start = ((), (), s32[]{:S(2)}) async-start(), calls=%async_computation.22 | async-start | bytes 3932160 | tf_op jit(solution)/shard_map/reduce_scatter | solution.py:270
  701.9 178.4 %reduce-scatter.21.cloned.1.call-start = ((), (), s32[]{:S(2)}) async-start(), calls=%async_computation.24 | async-start | bytes 3932160 | tf_op jit(solution)/shard_map/reduce_scatter | solution.py:294
  868.4 94.0 %reduce-scatter.25.cloned.1.call-start = ((), (), s32[]{:S(2)}) async-start(), calls=%async_computation.26 | async-start | bytes 3481600 | tf_op jit(solution)/shard_map/reduce_scatter | solution.py:314
  875.5 226.4 %all-reduce.3.cloned.1.call-start = ((), (), s32[]{:S(2)}) async-start(), calls=%async_computation.30 | async-start | bytes 180224 | tf_op jit(solution)/shard_map/psum | solution.py:332
  883.6 497.9 %reduce-scatter.27.cloned.1.call-start = ((), (), s32[]{:S(2)}) async-start(), calls=%async_computation.27 | async-start | bytes 13926400 | tf_op jit(solution)/shard_map/reduce_scatter | solution.py:311
  896.8 765.0 %reduce-scatter.29.cloned.1.call-start = ((), (), s32[]{:S(2)}) async-start(), calls=%async_computation.28 | async-start | bytes 13926400 | tf_op jit(solution)/shard_map/reduce_scatter | solution.py:315
  911.1 963.7 %reduce-scatter.23.cloned.1.call-start = ((), (), s32[]{:S(2)}) async-start(), calls=%async_computation.25 | async-start | bytes 10444800 | tf_op jit(solution)/shard_map/reduce_scatter | solution.py:310
  (67 other events, 2081.1 us)
Sparse Core Ops, SparseCore 0:
  24.9 12.3 all-gather.11
  159.6 36.2 all-gather.13
  198.0 38.9 all-gather.29
  239.6 58.1 all-gather.15
  303.1 10.5 reduce-scatter.10
  316.2 96.4 all-gather.19
  414.8 10.4 all-gather.17
  426.9 12.5 all-gather.23
  442.1 96.4 all-gather.21
  566.4 9.7 reduce-scatter.14
  580.5 9.7 reduce-scatter.12
  598.3 12.4 all-gather.25
  697.7 37.6 reduce-scatter.16
  738.0 82.2 all-gather.27
  823.0 35.4 reduce-scatter.18
  868.5 11.7 reduce-scatter.20
  883.1 79.2 reduce-scatter.24
  969.8 132.0 all-reduce.2
  1104.8 276.6 reduce-scatter.26
  1384.2 277.5 reduce-scatter.28
  1664.7 210.1 reduce-scatter.22
